TPU v7x, 32 devices: a whole 2x2x4 slice. The times are simulated.
32 devices in a mesh: groups: 2 (over x), steps: 8 (over z, y), inner: 2 (over core).
Axes of the slice: x: 2, y: 2, z: 4, core: 2. Of those that a mesh axis runs over, the one named last changes fastest.
Arguments:
- start_state: float32 [16, 32, 768], P('groups'), parts along dimension 0, may hold values from -6 to 6
- noise_draws: float32 [32, 8, 32, 768], P(('groups', 'steps', 'inner')), parts along dimension 0, may hold values from -6 to 6
- step_gaps: int32 [32], P(('groups', 'steps', 'inner')), parts along dimension 0, may hold values from 1 to 15
- window_start: int32 [2], P('groups'), parts along dimension 0, may hold values from 240 to 999
- input_weight: bfloat16 [768, 1024], replicated, may hold values from -0.21875 to 0.21875
- embed_weight: bfloat16 [256, 2048], replicated, may hold values from -0.375 to 0.375
- first_weight: bfloat16 [1024, 1024], replicated, may hold values from -0.1875 to 0.1875
- second_weight: bfloat16 [1024, 1024], replicated, may hold values from -0.1875 to 0.1875
- output_weight: bfloat16 [1024, 768], replicated, may hold values from -0.1875 to 0.1875
Outputs:
- trajectory: float32 [32, 8, 32, 768], P(('groups', 'steps', 'inner')), parts along dimension 0
There are 2 independent parts, one for each index of `groups`. A program takes and returns all parts, laid end to end along the dimension named above; an argument that names none is the same for every part. Nothing has to cross between parts.
All inputs are finite; a program needn't handle non-finite values.
Results may differ from a plain program's by a relative error of at most 0.00035.
Values sent between devices are 32-bit elements; how exact they have to be, the bound alone decides.
No kernel may reach another device: no remote copies, remote signals or barrier semaphores. Data moves between devices by JAX's collectives and lax.ppermute only.
A program may use at most 64 MiB of HBM per device.

v0:
```python
import math
import jax
import jax.numpy as jnp
from jax import lax
from jax.sharding import PartitionSpec as P

GROUPS = 32
ITERS = 2
TRAIN_STEPS = 1000
TIME = ("steps", "inner")


def noise_table():
    levels = jnp.arange(TRAIN_STEPS, dtype=jnp.float32)
    beta_values = 0.0001 + (0.02 - 0.0001) * levels / (TRAIN_STEPS - 1)
    return jnp.exp(jnp.cumsum(jnp.log1p(-beta_values)))


def lookup(table, levels):
    places = jnp.arange(TRAIN_STEPS, dtype=jnp.int32)
    return jnp.sum(jnp.where(places == levels[:, None], table, jnp.zeros_like(table)), axis=1)


def group_norm(hidden):
    times, patches, channels = hidden.shape

    def group_mean(values):
        per_channel = jnp.mean(values, axis=1).reshape(times, GROUPS, channels // GROUPS)
        per_group = jnp.mean(per_channel, axis=2, keepdims=True)
        return jnp.broadcast_to(per_group, per_channel.shape).reshape(times, 1, channels)

    offset = hidden - group_mean(hidden)
    return offset * lax.rsqrt(group_mean(offset * offset) + 1e-05)


def project(values, weight):
    return lax.dot_general(
        values.astype(jnp.bfloat16),
        weight,
        (((2,), (0,)), ((), ())),
        preferred_element_type=jnp.float32,
    )


def predict_noise(states, modulation, input_weight, first_weight, second_weight, output_weight):
    channels = input_weight.shape[1]
    scale_part = modulation[:, None, :channels]
    shift_part = modulation[:, None, channels:]
    entry = project(states, input_weight)
    act_one = jax.nn.silu(group_norm(entry) * (1.0 + scale_part) + shift_part)
    act_two = jax.nn.silu(group_norm(project(act_one, first_weight)))
    block = entry + project(act_two, second_weight)
    return project(jax.nn.silu(group_norm(block)), output_weight)


def shift_blocks(part, count, width, blocks):
    pairs = [(place, place + blocks * width) for place in range(count - blocks * width)]
    return lax.ppermute(part, TIME, pairs)


def earlier_blocks(part, count, width):
    total = shift_blocks(part, count, width, 1)
    reach = 1
    while reach < count // width - 1:
        total = total + shift_blocks(total, count, width, reach)
        reach *= 2
    return total


def shards(
    start_state,
    noise_draws,
    step_gaps,
    window_start,
    input_weight,
    embed_weight,
    first_weight,
    second_weight,
    output_weight,
):
    count = lax.axis_size(TIME)
    width = start_state.shape[0]
    assert count % width == 0
    groups = [list(range(first, first + width)) for first in range(0, count, width)]
    place = lax.axis_index(TIME)
    image = place % width
    first_time = place - image

    def exchange(values):
        return lax.all_to_all(values, TIME, 0, 0, axis_index_groups=groups, tiled=True)

    noise = exchange(noise_draws[0])
    later = jnp.arange(count + 1, dtype=jnp.int32) > place
    before = lax.psum(jnp.where(later, step_gaps[0], 0), TIME)
    marks = window_start[0] - lax.dynamic_slice_in_dim(before, first_time, width + 1)
    bars = lookup(noise_table(), marks)
    bar_now = bars[:-1, None, None]
    bar_next = bars[1:, None, None]
    half = embed_weight.shape[0] // 2
    frequency = jnp.exp(-math.log(10000.0) * jnp.arange(half, dtype=jnp.float32) / half)
    angles = marks[:-1, None].astype(jnp.float32) * frequency
    features = jnp.concatenate([jnp.cos(angles), jnp.sin(angles)], axis=1).astype(jnp.bfloat16)
    modulation = jnp.dot(features, embed_weight, preferred_element_type=jnp.float32)
    sigma = jnp.sqrt((1.0 - bar_next) / (1.0 - bar_now) * (1.0 - bar_now / bar_next))
    noise_coef = (1.0 - bar_next) * jnp.sqrt(bar_now / (bar_next * (1.0 - bar_now)))
    own = lax.dynamic_index_in_dim(start_state, image, 0, True)
    states = own
    for iteration in range(ITERS):
        predicted = predict_noise(
            states, modulation, input_weight, first_weight, second_weight, output_weight
        )
        clean = jnp.clip(
            (states - jnp.sqrt(1.0 - bar_now) * predicted) / jnp.sqrt(bar_now), -1.0, 1.0
        )
        implied = (states - jnp.sqrt(bar_now) * clean) / jnp.sqrt(1.0 - bar_now)
        drift = jnp.sqrt(bar_next) * clean + noise_coef * implied + sigma * noise - states
        totals = jnp.cumsum(drift, axis=0)
        base = own + earlier_blocks(totals[-1:], count, width)
        states = base + (totals - drift)
    return exchange(states + drift)[None]


def solution(mesh):
    return jax.shard_map(
        shards,
        mesh=mesh,
        in_specs=(
            P("groups", None, None),
            P(("groups", "steps", "inner"), None, None, None),
            P(("groups", "steps", "inner")),
            P("groups"),
            P(),
            P(),
            P(),
            P(),
            P(),
        ),
        out_specs=P(("groups", "steps", "inner"), None, None, None),
        check_vma=False,
    )
```

profile of v0, /device:TPU:0, one launch (start us, length us, event | category | flops | bytes accessed | tf_op | source)
XLA Modules:
  0.0 87.1 jit_solution(368406443984099906)
XLA Ops:
  0.0 5.4 %all-to-all-start = ((f32[8,32,768]{2,1,0:T(8,128)}), f32[8,32,768]{2,1,0:T(8,128)}, u32[]{:S(2)}, u32[]{:S(2)}) async-start(f32[8,32,768]{2,1,0:T(8,128)} %bitcast.78), calls=%async_computation | async-start | bytes 1572864 | tf_op jit(solution)/shard_map/all_to_all | solution.py:90
  6.8 18.0 %psum.7 = s32[17]{0:T(128)S(1)} all-reduce(s32[17]{0:T(128)S(1)} %compare_select_fusion), channel_id=1, replica_groups=mesh['groups'=2,'steps'=8,'inner'=2] {'steps','inner'}, use_global_device_ids=true, to_apply=%region_0.1 | all-reduce | flops 17 | bytes 136 | tf_op jit(solution)/shard_map/psum | solution.py:94
  24.9 0.3 reduce-window.9
  25.2 0.1 fusion.73
  25.4 1.5 %fusion.75 = f32[8,2048]{1,0:T(8,128)S(1)} fusion(bf16[256,2048]{1,0:T(8,128)(2,1)} %param.14, bf16[8,128]{1,0:T(8,128)(2,1)S(1)} %get-tuple-element.8, bf16[8,128]{1,0:T(8,128)(2,1)S(1)} %get-tuple-element.7), kind=kOutput, calls=%fused_computation.87 | convolution fusion | flops 8396800 | bytes 1118208 | tf_op jit(solution)/shard_map/dot_general | solution.py:103
  26.8 1.9 %fusion.88 = (f32[1024]{0:T(1024)S(1)}, f32[32,1024]{1,0:T(8,128)S(1)}) fusion(bf16[768,1024]{1,0:T(8,128)(2,1)} %param.13, f32[8,32,768]{2,1,0:T(8,128)} %param.9, s32[]{:T(128)S(6)} %select_n.23), kind=kOutput, calls=%fused_computation.128 | convolution fusion | flops 50363392 | bytes 1757188 | tf_op jit(solution)/shard_map/dot_general | solution.py:37
  28.8 0.1 reduce_sum.227
  29.2 0.1 reduce_sum.229
  29.5 0.8 fusion.89
  30.3 0.1 div.177
  30.4 0.1 reduce_sum.231
  30.6 0.1 sub.131
  30.8 0.2 multiply_reduce_fusion.4
  31.0 0.1 reduce_sum.233
  31.2 0.1 broadcast_in_dim.52
  31.3 0.1 rsqrt.75
  31.4 2.7 %fusion.90 = (f32[8,1024]{1,0:T(8,128)S(1)}, f32[8,32,1024]{2,1,0:T(8,128)S(1)}) fusion(bf16[1024,1024]{1,0:T(8,128)(2,1)} %param.16, f32[8,32,1024]{2,1,0:T(8,128)} %copy-done.5, f32[8,1024]{1,0:T(8,128)S(1)} %rsqrt.75, f32[8,1024]{1,0:T(8,128)S(1)} %sub.131, f32[32,1024]{1,0:T(8,128)S(1)} %get-tuple-element.15), kind=kOutput, calls=%fused_computation.130 | convolution fusion | flops 539222016 | bytes 4423680 | tf_op jit(solution)/shard_map/dot_general | solution.py:37
  34.1 0.1 div.184
  34.2 0.1 reduce_sum.235
  34.4 0.1 sub.134
  34.5 0.2 multiply_reduce_fusion.3
  34.7 0.1 div.187
  34.8 0.1 reduce_sum.237
  35.0 0.1 broadcast_in_dim.54
  35.1 0.1 rsqrt.77
  35.2 0.1 slice_reduce_fusion
  35.4 0.2 select_reduce_fusion
  35.6 0.9 %dynamic-slice_bitcast_fusion = f32[32,768]{1,0:T(8,128)S(1)} fusion(f32[8,32,768]{2,1,0:T(8,128)} %param.9, s32[]{:T(128)S(6)} %select_n.23), kind=kLoop, calls=%fused_computation.66 | loop fusion | bytes 196612 | tf_op jit(solution)/shard_map/sub | solution.py:113
  36.6 2.5 %add_subtract_fusion.1 = f32[8,32,768]{2,1,0:T(8,128)S(1)} fusion(bf16[1024,768]{1,0:T(8,128)(2,1)} %param.17, f32[8,32,768]{2,1,0:T(8,128)} %all-to-all-done, f32[8,32,1024]{2,1,0:T(8,128)S(1)} %get-tuple-element.19, f32[8,1024]{1,0:T(8,128)S(1)} %rsqrt.77, f32[8,1024]{1,0:T(8,128)S(1)} %sub.134, f32[8]{0:T(128)S(1)} %get-tuple-element.11, ...), kind=kOutput, calls=%fused_computation.38 | convolution fusion | flops 407044096 | bytes 4358304 | tf_op jit(solution)/shard_map/dot_general | solution.py:37
  39.1 1.7 %fusion.94 = f32[8,32,768]{2,1,0:T(8,128)S(1)} fusion(f32[8,32,768]{2,1,0:T(8,128)S(1)} %add_subtract_fusion.1), kind=kOutput, calls=%fused_computation.134 | output fusion | flops 1376256 | bytes 1572864 | tf_op jit(solution)/shard_map/jit(cumsum)/reduce_window_sum | solution.py:117
  40.8 1.9 %collective-permute-start = (f32[1,32,768]{2,1,0:T(8,128)S(1)}, f32[1,32,768]{2,1,0:T(8,128)S(1)}, u32[]{:S(2)}, u32[]{:S(2)}) collective-permute-start(f32[1,32,768]{2,1,0:T(8,128)S(1)} %slice.46), channel_id=1, source_target_pairs={{0,8},{1,9},{2,10},{3,11},{4,12},{5,13},{6,14},{7,15},{16,24},{17,... | collective-permute-start | bytes 294920 | tf_op jit(solution)/shard_map/ppermute | solution.py:58
  42.7 2.2 %collective-permute-done = f32[1,32,768]{2,1,0:T(8,128)S(1)} collective-permute-done((f32[1,32,768]{2,1,0:T(8,128)S(1)}, f32[1,32,768]{2,1,0:T(8,128)S(1)}, u32[]{:S(2)}, u32[]{:S(2)}) %collective-permute-start) | collective-permute-done | bytes 98336 | tf_op jit(solution)/shard_map/ppermute | solution.py:58
  44.9 0.9 %add_bitcast_fusion.1 = f32[32,768]{1,0:T(8,128)S(1)} fusion(f32[1,32,768]{2,1,0:T(8,128)S(1)} %collective-permute-done, f32[8,32,768]{2,1,0:T(8,128)} %param.9, s32[]{:T(128)S(6)} %select_n.23), kind=kLoop, calls=%fused_computation.64 | loop fusion | flops 24576 | bytes 294916 | tf_op jit(solution)/shard_map/add | solution.py:119
  45.8 0.6 fusion.91
  46.5 0.1 reduce_sum.239
  46.8 0.1 sub.143
  46.9 0.2 multiply_reduce_fusion.2
  47.2 0.1 reduce_sum.241
  47.3 0.1 broadcast_in_dim.56
  47.4 0.1 rsqrt.79
  47.5 1.9 %fusion.92 = (f32[8,1024]{1,0:T(8,128)S(1)}, f32[8,32,1024]{2,1,0:T(8,128)}) fusion(bf16[1024,1024]{1,0:T(8,128)(2,1)S(1)} %copy-done, f32[8,32,1024]{2,1,0:T(8,128)S(1)} %get-tuple-element.21, f32[8,1024]{1,0:T(8,128)S(1)} %rsqrt.79, f32[8,1024]{1,0:T(8,128)S(1)} %sub.143, f32[8,1024]{1,0:T(8,128)S(1)} %get-tuple-element.6, ...), kind=kOutput, calls=%fused_computation.132 | convolution fusion | flops 539484160 | bytes 4358144 | tf_op jit(solution)/shard_map/dot_general | solution.py:37
  49.4 0.1 div.204
  49.5 0.1 reduce_sum.243
  49.7 0.1 sub.146
  49.8 1.4 %multiply_reduce_fusion.1 = f32[8,1024]{1,0:T(8,128)S(1)} fusion(f32[8,32,1024]{2,1,0:T(8,128)} %get-tuple-element.23, f32[8,1024]{1,0:T(8,128)S(1)} %sub.146), kind=kLoop, calls=%fused_computation.27 | loop fusion | flops 778240 | bytes 1114112 | tf_op jit(solution)/shard_map/reduce_sum | solution.py:28
  51.3 0.1 reduce_sum.245
  51.5 0.1 broadcast_in_dim.58
  51.6 0.1 rsqrt.81
  51.7 3.7 %fusion.93 = (f32[8,1024]{1,0:T(8,128)S(1)}, f32[8,32,1024]{2,1,0:T(8,128)}) fusion(f32[8,32,1024]{2,1,0:T(8,128)S(1)} %get-tuple-element.21, bf16[1024,1024]{1,0:T(8,128)(2,1)} %param.16, f32[8,32,1024]{2,1,0:T(8,128)} %get-tuple-element.23, f32[8,1024]{1,0:T(8,128)S(1)} %rsqrt.81, f32[8,1024]{1,0:T(8,128)S(1)} %sub.146), kind=kOutput, calls=%fused_computation.133 | convolution fusion | flops 539222016 | bytes 5341184 | tf_op jit(solution)/shard_map/dot_general | solution.py:37
  55.4 0.1 div.211
  55.5 0.1 reduce_sum.247
  55.7 0.1 sub.149
  55.8 1.4 %multiply_reduce_fusion = f32[8,1024]{1,0:T(8,128)S(1)} fusion(f32[8,32,1024]{2,1,0:T(8,128)} %get-tuple-element.25, f32[8,1024]{1,0:T(8,128)S(1)} %sub.149), kind=kLoop, calls=%fused_computation.25 | loop fusion | flops 778240 | bytes 1114112 | tf_op jit(solution)/shard_map/reduce_sum | solution.py:28
  57.3 0.1 reduce_sum.249
  57.4 0.1 broadcast_in_dim.60
  57.5 0.1 rsqrt.83
  57.7 3.1 %add_subtract_fusion = f32[8,32,768]{2,1,0:T(8,128)S(1)} fusion(bf16[1024,768]{1,0:T(8,128)(2,1)} %param.17, f32[8,32,768]{2,1,0:T(8,128)} %all-to-all-done, f32[8,32,1024]{2,1,0:T(8,128)} %get-tuple-element.25, f32[8,1024]{1,0:T(8,128)S(1)} %rsqrt.83, f32[8,1024]{1,0:T(8,128)S(1)} %sub.149, f32[8]{0:T(128)S(1)} %get-tuple-element.11, ...), kind=kOutput, calls=%fused_computation.36 | convolution fusion | flops 407437312 | bytes 5931168 | tf_op jit(solution)/shard_map/dot_general | solution.py:37
  60.7 1.7 %fusion.95 = f32[8,32,768]{2,1,0:T(8,128)S(1)} fusion(f32[8,32,768]{2,1,0:T(8,128)S(1)} %add_subtract_fusion), kind=kOutput, calls=%fused_computation.135 | output fusion | flops 1376256 | bytes 1572864 | tf_op jit(solution)/shard_map/jit(cumsum)/reduce_window_sum | solution.py:117
  62.4 5.3 %collective-permute-start.1 = (f32[1,32,768]{2,1,0:T(8,128)S(1)}, f32[1,32,768]{2,1,0:T(8,128)S(1)}, u32[]{:S(2)}, u32[]{:S(2)}) collective-permute-start(f32[1,32,768]{2,1,0:T(8,128)S(1)} %slice.47), channel_id=1, source_target_pairs={{0,8},{1,9},{2,10},{3,11},{4,12},{5,13},{6,14},{7,15},{16,24},{17,... | collective-permute-start | bytes 294920 | tf_op jit(solution)/shard_map/ppermute | solution.py:58
  67.8 2.2 %collective-permute-done.1 = f32[1,32,768]{2,1,0:T(8,128)S(1)} collective-permute-done((f32[1,32,768]{2,1,0:T(8,128)S(1)}, f32[1,32,768]{2,1,0:T(8,128)S(1)}, u32[]{:S(2)}, u32[]{:S(2)}) %collective-permute-start.1) | collective-permute-done | bytes 98336 | tf_op jit(solution)/shard_map/ppermute | solution.py:58
  69.9 0.9 %add_bitcast_fusion = f32[32,768]{1,0:T(8,128)S(1)} fusion(f32[1,32,768]{2,1,0:T(8,128)S(1)} %collective-permute-done.1, f32[8,32,768]{2,1,0:T(8,128)} %param.9, s32[]{:T(128)S(6)} %select_n.23), kind=kLoop, calls=%fused_computation.63 | loop fusion | flops 24576 | bytes 294916 | tf_op jit(solution)/shard_map/add | solution.py:119
  70.8 0.1 add_add_fusion
  71.0 15.3 %all_to_all.10 = f32[8,32,768]{2,1,0:T(8,128)S(1)} all-to-all(f32[8,32,768]{2,1,0:T(8,128)S(1)} %add_add_fusion), channel_id=1, replica_groups={{0,1,2,3,4,5,6,7},{8,9,10,11,12,13,14,15},{16,17,18,19,20,21,22,23},{24..., dimensions={0} | all-to-all | bytes 1572864 | tf_op jit(solution)/shard_map/all_to_all | solution.py:90
  86.3 0.9 %copy.13 = f32[1,8,32,768]{3,2,1,0:T(8,128)} copy(f32[1,8,32,768]{3,2,1,0:T(8,128)S(1)} %bitcast.77) | data formatting | bytes 1572864
  (69 shorter events, 2.0 us)
Async XLA Ops:
  0.0 29.5 %copy-start = (bf16[1024,1024]{1,0:T(8,128)(2,1)S(1)}, bf16[1024,1024]{1,0:T(8,128)(2,1)}, u32[]{:S(2)}) copy-start(bf16[1024,1024]{1,0:T(8,128)(2,1)} %param.15) | copy-start | bytes 6291460
  0.0 36.6 %all-to-all-start = ((f32[8,32,768]{2,1,0:T(8,128)}), f32[8,32,768]{2,1,0:T(8,128)}, u32[]{:S(2)}, u32[]{:S(2)}) async-start(f32[8,32,768]{2,1,0:T(8,128)} %bitcast.78), calls=%async_computation | async-start | bytes 1572864 | tf_op jit(solution)/shard_map/all_to_all | solution.py:90
  30.3 1.0 %copy-start.5 = (f32[8,32,1024]{2,1,0:T(8,128)}, f32[8,32,1024]{2,1,0:T(8,128)S(1)}, u32[]{:S(2)}) copy-start(f32[8,32,1024]{2,1,0:T(8,128)S(1)} %get-tuple-element.17) | copy-start | bytes 3145732
  39.0 7.4 %copy-start.4 = (f32[8,32,768]{2,1,0:T(8,128)}, f32[8,32,768]{2,1,0:T(8,128)S(1)}, u32[]{:S(2)}) copy-start(f32[8,32,768]{2,1,0:T(8,128)S(1)} %add_subtract_fusion.1) | copy-start | bytes 2359300
  39.1 6.8 %copy-start.1 = (bf16[768,1024]{1,0:T(8,128)(2,1)S(1)}, bf16[768,1024]{1,0:T(8,128)(2,1)}, u32[]{:S(2)}) copy-start(bf16[768,1024]{1,0:T(8,128)(2,1)} %param.13) | copy-start | bytes 4718596
  40.8 5.7 %copy-start.2 = (f32[8,32,768]{2,1,0:T(8,128)}, f32[8,32,768]{2,1,0:T(8,128)S(1)}, u32[]{:S(2)}) copy-start(f32[8,32,768]{2,1,0:T(8,128)S(1)} %fusion.94) | copy-start | bytes 2359300
  40.8 4.1 %collective-permute-start = (f32[1,32,768]{2,1,0:T(8,128)S(1)}, f32[1,32,768]{2,1,0:T(8,128)S(1)}, u32[]{:S(2)}, u32[]{:S(2)}) collective-permute-start(f32[1,32,768]{2,1,0:T(8,128)S(1)} %slice.46), channel_id=1, source_target_pairs={{0,8},{1,9},{2,10},{3,11},{4,12},{5,13},{6,14},{7,15},{16,24},{17,... | collective-permute-start | bytes 294920 | tf_op jit(solution)/shard_map/ppermute | solution.py:58
  55.4 2.3 %copy-start.3 = (f32[8,32,768]{2,1,0:T(8,128)S(1)}, f32[8,32,768]{2,1,0:T(8,128)}, u32[]{:S(2)}) copy-start(f32[8,32,768]{2,1,0:T(8,128)} %copy-done.2) | copy-start | bytes 2359300
  62.4 7.5 %collective-permute-start.1 = (f32[1,32,768]{2,1,0:T(8,128)S(1)}, f32[1,32,768]{2,1,0:T(8,128)S(1)}, u32[]{:S(2)}, u32[]{:S(2)}) collective-permute-start(f32[1,32,768]{2,1,0:T(8,128)S(1)} %slice.47), channel_id=1, source_target_pairs={{0,8},{1,9},{2,10},{3,11},{4,12},{5,13},{6,14},{7,15},{16,24},{17,... | collective-permute-start | bytes 294920 | tf_op jit(solution)/shard_map/ppermute | solution.py:58
where the time goes:
time: 87.7 us; the launch traced here: 87.1 us
  blocking collectives  33.3 us (38%)
  matrix products  18.5 us (21%)
  starting transfers between devices  12.6 us (14%)
  other arithmetic  11 us (13%)
  local copies, waits for them, and re-layouts  5.39 us (6%)
  waiting for transfers between devices  4.38 us (5%)
  between operations  1.9 us (2%)
    psum x1, blocking collectives, shards(): before = lax.psum(jnp.where(later, step_gaps[0], 0), TIME)  18 us
    dot_general x8, matrix products, project(): lax.dot_general(values.astype(jnp.bfloat16), weight, (((2,), (0,)), ((),...  17.1 us
    all_to_all x1, blocking collectives, exchange(): lax.all_to_all(values, TIME, 0, 0, axis_index_groups=groups, tiled=True)  15.3 us
    ppermute x2, starting transfers between devices, shift_blocks(): return lax.ppermute(part, TIME, pairs)  7.21 us
    all_to_all x1, starting transfers between devices, exchange(): lax.all_to_all(values, TIME, 0, 0, axis_index_groups=groups, tiled=True)  5.42 us
    ppermute x2, waiting for transfers between devices, shift_blocks(): return lax.ppermute(part, TIME, pairs)  4.38 us
    another operation x2, other arithmetic, shards(): totals = jnp.cumsum(drift, axis=0)  3.39 us
    reduce_sum x6, other arithmetic, group_mean(): jnp.mean(values, axis=1).reshape(times, GROUPS, channels // GROUPS)  3.38 us
  transfers between devices with their start and end apart: 3, of which 2 were waited for; matrix products, arithmetic and copies ran while one was open for 13% of the time, Pallas kernels for 0%

commit v1 on v0

--- a/solution.py
+++ b/solution.py
@@ -91,7 +91,9 @@
 
     noise = exchange(noise_draws[0])
     later = jnp.arange(count + 1, dtype=jnp.int32) > place
-    before = lax.psum(jnp.where(later, step_gaps[0], 0), TIME)
+    x = jnp.where(later, step_gaps[0], 0)
+    pieces = lax.all_gather(x, TIME)
+    before = jnp.sum(pieces, axis=0)
     marks = window_start[0] - lax.dynamic_slice_in_dim(before, first_time, width + 1)
     bars = lookup(noise_table(), marks)
     bar_now = bars[:-1, None, None]

time: 87.7 us -> 95.7 us (1.091)
  blocking collectives: 33.3 us -> 41.2 us
    all_gather x0 -> x1, blocking collectives: none -> 24 us  [shards(): pieces = lax.all_gather(x, TIME)]
    psum x1 -> x0, blocking collectives: 18 us -> none  [shards(): before = lax.psum(jnp.where(later, step_gaps[0], 0), TIME)]
    all_to_all x1, blocking collectives: 15.3 us -> 17.2 us  [exchange(): lax.all_to_all(values, TIME, 0, 0, axis_index_groups=groups, tiled=True)]
  transfers between devices with their start and end apart: 3 -> 3, of which waited for: 2 -> 2; matrix products, arithmetic and copies ran while one was open for 13% -> 12% of each run, Pallas kernels for 0% -> 0%
where the time goes in v1:
time: 95.7 us; the launch traced here: 95.2 us
  blocking collectives  41.2 us (43%)
  matrix products  18.5 us (19%)
  starting transfers between devices  12.1 us (13%)
  other arithmetic  11.1 us (12%)
  local copies, waits for them, and re-layouts  5.39 us (6%)
  waiting for transfers between devices  5.05 us (5%)
  between operations  1.91 us (2%)
    all_gather x1, blocking collectives, shards(): pieces = lax.all_gather(x, TIME)  24 us
    all_to_all x1, blocking collectives, exchange(): lax.all_to_all(values, TIME, 0, 0, axis_index_groups=groups, tiled=True)  17.2 us
    dot_general x8, matrix products, project(): lax.dot_general(values.astype(jnp.bfloat16), weight, (((2,), (0,)), ((),...  17 us
    ppermute x2, starting transfers between devices, shift_blocks(): return lax.ppermute(part, TIME, pairs)  6.66 us
    all_to_all x1, starting transfers between devices, exchange(): lax.all_to_all(values, TIME, 0, 0, axis_index_groups=groups, tiled=True)  5.42 us
    ppermute x2, waiting for transfers between devices, shift_blocks(): return lax.ppermute(part, TIME, pairs)  5.04 us
    another operation x2, other arithmetic, shards(): totals = jnp.cumsum(drift, axis=0)  3.39 us
    reduce_sum x6, other arithmetic, group_mean(): jnp.mean(values, axis=1).reshape(times, GROUPS, channels // GROUPS)  3.38 us
  transfers between devices with their start and end apart: 3, of which 2 were waited for; matrix products, arithmetic and copies ran while one was open for 12% of the time, Pallas kernels for 0%

profile of v1, /device:TPU:0, one launch (start us, length us, event | category | flops | bytes accessed | tf_op | source)
XLA Modules:
  0.0 95.2 jit_solution(16028556573466421383)
XLA Ops:
  0.0 5.4 %all-to-all-start = ((f32[8,32,768]{2,1,0:T(8,128)}), f32[8,32,768]{2,1,0:T(8,128)}, u32[]{:S(2)}, u32[]{:S(2)}) async-start(f32[8,32,768]{2,1,0:T(8,128)} %bitcast.80), calls=%async_computation | async-start | bytes 1572864 | tf_op jit(solution)/shard_map/all_to_all | solution.py:90
  6.8 0.3 reduce-window.9
  7.2 24.0 %all-gather = s32[16,1,17]{2,1,0:T(1,128)S(1)} all-gather(s32[1,1,17]{2,1,0:T(1,128)S(1)} %fusion.79), channel_id=1, replica_groups=mesh['groups'=2,'steps'=8,'inner'=2] {'steps','inner'}, dimensions={0}, use_global_device_ids=true | all-gather | bytes 1156 | tf_op jit(solution)/shard_map/all_gather | solution.py:95
  31.3 0.1 fusion.73
  31.4 1.5 %fusion.75 = f32[8,2048]{1,0:T(8,128)S(1)} fusion(bf16[256,2048]{1,0:T(8,128)(2,1)} %param.14, bf16[8,128]{1,0:T(8,128)(2,1)S(1)} %get-tuple-element.8, bf16[8,128]{1,0:T(8,128)(2,1)S(1)} %get-tuple-element.7), kind=kOutput, calls=%fused_computation.87 | convolution fusion | flops 8396800 | bytes 1118208 | tf_op jit(solution)/shard_map/dot_general | solution.py:105
  32.9 1.9 %fusion.89 = (f32[1024]{0:T(1024)S(1)}, f32[32,1024]{1,0:T(8,128)S(1)}) fusion(bf16[768,1024]{1,0:T(8,128)(2,1)} %param.13, f32[8,32,768]{2,1,0:T(8,128)} %param.9, s32[]{:T(128)S(6)} %select_n.30), kind=kOutput, calls=%fused_computation.129 | convolution fusion | flops 50363392 | bytes 1757188 | tf_op jit(solution)/shard_map/dot_general | solution.py:37
  34.8 0.1 reduce_sum.237
  35.2 0.1 reduce_sum.239
  35.5 0.8 fusion.90
  36.3 0.1 div.177
  36.4 0.1 reduce_sum.241
  36.7 0.1 sub.131
  36.8 0.2 multiply_reduce_fusion.4
  37.1 0.1 reduce_sum.243
  37.2 0.1 broadcast_in_dim.52
  37.3 0.1 rsqrt.75
  37.4 2.7 %fusion.91 = (f32[8,1024]{1,0:T(8,128)S(1)}, f32[8,32,1024]{2,1,0:T(8,128)S(1)}) fusion(bf16[1024,1024]{1,0:T(8,128)(2,1)} %param.16, f32[8,32,1024]{2,1,0:T(8,128)} %copy-done.5, f32[8,1024]{1,0:T(8,128)S(1)} %rsqrt.75, f32[8,1024]{1,0:T(8,128)S(1)} %sub.131, f32[32,1024]{1,0:T(8,128)S(1)} %get-tuple-element.15), kind=kOutput, calls=%fused_computation.131 | convolution fusion | flops 539222016 | bytes 4423680 | tf_op jit(solution)/shard_map/dot_general | solution.py:37
  40.1 0.1 div.184
  40.2 0.1 reduce_sum.245
  40.5 0.1 sub.134
  40.6 0.2 multiply_reduce_fusion.3
  40.8 0.1 div.187
  40.9 0.1 reduce_sum.247
  41.0 0.1 broadcast_in_dim.54
  41.1 0.1 rsqrt.77
  41.2 0.1 slice_reduce_fusion
  41.4 0.2 select_reduce_fusion
  41.6 0.9 dynamic-slice_bitcast_fusion
  42.6 2.5 %add_subtract_fusion.1 = f32[8,32,768]{2,1,0:T(8,128)S(1)} fusion(bf16[1024,768]{1,0:T(8,128)(2,1)} %param.17, f32[8,32,768]{2,1,0:T(8,128)} %all-to-all-done, f32[8,32,1024]{2,1,0:T(8,128)S(1)} %get-tuple-element.19, f32[8,1024]{1,0:T(8,128)S(1)} %rsqrt.77, f32[8,1024]{1,0:T(8,128)S(1)} %sub.134, f32[8]{0:T(128)S(1)} %get-tuple-element.11, ...), kind=kOutput, calls=%fused_computation.38 | convolution fusion | flops 407044096 | bytes 4358304 | tf_op jit(solution)/shard_map/dot_general | solution.py:37
  45.1 1.7 %fusion.95 = f32[8,32,768]{2,1,0:T(8,128)S(1)} fusion(f32[8,32,768]{2,1,0:T(8,128)S(1)} %add_subtract_fusion.1), kind=kOutput, calls=%fused_computation.135 | output fusion | flops 1376256 | bytes 1572864 | tf_op jit(solution)/shard_map/jit(cumsum)/reduce_window_sum | solution.py:119
  46.8 1.3 %collective-permute-start = (f32[1,32,768]{2,1,0:T(8,128)S(1)}, f32[1,32,768]{2,1,0:T(8,128)S(1)}, u32[]{:S(2)}, u32[]{:S(2)}) collective-permute-start(f32[1,32,768]{2,1,0:T(8,128)S(1)} %slice.46), channel_id=1, source_target_pairs={{0,8},{1,9},{2,10},{3,11},{4,12},{5,13},{6,14},{7,15},{16,24},{17,... | collective-permute-start | bytes 294920 | tf_op jit(solution)/shard_map/ppermute | solution.py:58
  48.1 2.9 %collective-permute-done = f32[1,32,768]{2,1,0:T(8,128)S(1)} collective-permute-done((f32[1,32,768]{2,1,0:T(8,128)S(1)}, f32[1,32,768]{2,1,0:T(8,128)S(1)}, u32[]{:S(2)}, u32[]{:S(2)}) %collective-permute-start) | collective-permute-done | bytes 98336 | tf_op jit(solution)/shard_map/ppermute | solution.py:58
  51.0 0.9 add_bitcast_fusion.1
  51.9 0.6 fusion.92
  52.6 0.1 reduce_sum.249
  52.8 0.1 sub.143
  53.0 0.2 multiply_reduce_fusion.2
  53.2 0.1 reduce_sum.251
  53.4 0.1 broadcast_in_dim.56
  53.5 0.1 rsqrt.79
  53.6 1.9 %fusion.93 = (f32[8,1024]{1,0:T(8,128)S(1)}, f32[8,32,1024]{2,1,0:T(8,128)}) fusion(bf16[1024,1024]{1,0:T(8,128)(2,1)S(1)} %copy-done, f32[8,32,1024]{2,1,0:T(8,128)S(1)} %get-tuple-element.21, f32[8,1024]{1,0:T(8,128)S(1)} %rsqrt.79, f32[8,1024]{1,0:T(8,128)S(1)} %sub.143, f32[8,1024]{1,0:T(8,128)S(1)} %get-tuple-element.6, ...), kind=kOutput, calls=%fused_computation.133 | convolution fusion | flops 539484160 | bytes 4358144 | tf_op jit(solution)/shard_map/dot_general | solution.py:37
  55.5 0.1 div.204
  55.6 0.1 reduce_sum.253
  55.8 0.1 sub.146
  55.9 1.4 %multiply_reduce_fusion.1 = f32[8,1024]{1,0:T(8,128)S(1)} fusion(f32[8,32,1024]{2,1,0:T(8,128)} %get-tuple-element.23, f32[8,1024]{1,0:T(8,128)S(1)} %sub.146), kind=kLoop, calls=%fused_computation.27 | loop fusion | flops 778240 | bytes 1114112 | tf_op jit(solution)/shard_map/reduce_sum | solution.py:28
  57.4 0.1 reduce_sum.255
  57.5 0.1 broadcast_in_dim.58
  57.6 0.1 rsqrt.81
  57.8 3.7 %fusion.94 = (f32[8,1024]{1,0:T(8,128)S(1)}, f32[8,32,1024]{2,1,0:T(8,128)}) fusion(f32[8,32,1024]{2,1,0:T(8,128)S(1)} %get-tuple-element.21, bf16[1024,1024]{1,0:T(8,128)(2,1)} %param.16, f32[8,32,1024]{2,1,0:T(8,128)} %get-tuple-element.23, f32[8,1024]{1,0:T(8,128)S(1)} %rsqrt.81, f32[8,1024]{1,0:T(8,128)S(1)} %sub.146), kind=kOutput, calls=%fused_computation.134 | convolution fusion | flops 539222016 | bytes 5341184 | tf_op jit(solution)/shard_map/dot_general | solution.py:37
  61.4 0.1 div.211
  61.5 0.1 reduce_sum.257
  61.8 0.1 sub.149
  61.9 1.4 %multiply_reduce_fusion = f32[8,1024]{1,0:T(8,128)S(1)} fusion(f32[8,32,1024]{2,1,0:T(8,128)} %get-tuple-element.25, f32[8,1024]{1,0:T(8,128)S(1)} %sub.149), kind=kLoop, calls=%fused_computation.25 | loop fusion | flops 778240 | bytes 1114112 | tf_op jit(solution)/shard_map/reduce_sum | solution.py:28
  63.4 0.1 reduce_sum.259
  63.5 0.1 broadcast_in_dim.60
  63.6 0.1 rsqrt.83
  63.7 3.1 %add_subtract_fusion = f32[8,32,768]{2,1,0:T(8,128)S(1)} fusion(bf16[1024,768]{1,0:T(8,128)(2,1)} %param.17, f32[8,32,768]{2,1,0:T(8,128)} %all-to-all-done, f32[8,32,1024]{2,1,0:T(8,128)} %get-tuple-element.25, f32[8,1024]{1,0:T(8,128)S(1)} %rsqrt.83, f32[8,1024]{1,0:T(8,128)S(1)} %sub.149, f32[8]{0:T(128)S(1)} %get-tuple-element.11, ...), kind=kOutput, calls=%fused_computation.36 | convolution fusion | flops 407437312 | bytes 5931168 | tf_op jit(solution)/shard_map/dot_general | solution.py:37
  66.8 1.7 %fusion.96 = f32[8,32,768]{2,1,0:T(8,128)S(1)} fusion(f32[8,32,768]{2,1,0:T(8,128)S(1)} %add_subtract_fusion), kind=kOutput, calls=%fused_computation.136 | output fusion | flops 1376256 | bytes 1572864 | tf_op jit(solution)/shard_map/jit(cumsum)/reduce_window_sum | solution.py:119
  68.5 5.4 %collective-permute-start.1 = (f32[1,32,768]{2,1,0:T(8,128)S(1)}, f32[1,32,768]{2,1,0:T(8,128)S(1)}, u32[]{:S(2)}, u32[]{:S(2)}) collective-permute-start(f32[1,32,768]{2,1,0:T(8,128)S(1)} %slice.47), channel_id=1, source_target_pairs={{0,8},{1,9},{2,10},{3,11},{4,12},{5,13},{6,14},{7,15},{16,24},{17,... | collective-permute-start | bytes 294920 | tf_op jit(solution)/shard_map/ppermute | solution.py:58
  73.9 2.2 %collective-permute-done.1 = f32[1,32,768]{2,1,0:T(8,128)S(1)} collective-permute-done((f32[1,32,768]{2,1,0:T(8,128)S(1)}, f32[1,32,768]{2,1,0:T(8,128)S(1)}, u32[]{:S(2)}, u32[]{:S(2)}) %collective-permute-start.1) | collective-permute-done | bytes 98336 | tf_op jit(solution)/shard_map/ppermute | solution.py:58
  76.1 0.9 add_bitcast_fusion
  77.0 0.1 add_add_fusion
  77.1 17.2 %all_to_all.10 = f32[8,32,768]{2,1,0:T(8,128)S(1)} all-to-all(f32[8,32,768]{2,1,0:T(8,128)S(1)} %add_add_fusion), channel_id=1, replica_groups={{0,1,2,3,4,5,6,7},{8,9,10,11,12,13,14,15},{16,17,18,19,20,21,22,23},{24..., dimensions={0} | all-to-all | bytes 1572864 | tf_op jit(solution)/shard_map/all_to_all | solution.py:90
  94.3 0.9 copy.13
  (70 shorter events, 2.0 us)
Async XLA Ops:
  0.0 35.5 %copy-start = (bf16[1024,1024]{1,0:T(8,128)(2,1)S(1)}, bf16[1024,1024]{1,0:T(8,128)(2,1)}, u32[]{:S(2)}) copy-start(bf16[1024,1024]{1,0:T(8,128)(2,1)} %param.15) | copy-start | bytes 6291460
  0.0 42.6 %all-to-all-start = ((f32[8,32,768]{2,1,0:T(8,128)}), f32[8,32,768]{2,1,0:T(8,128)}, u32[]{:S(2)}, u32[]{:S(2)}) async-start(f32[8,32,768]{2,1,0:T(8,128)} %bitcast.80), calls=%async_computation | async-start | bytes 1572864 | tf_op jit(solution)/shard_map/all_to_all | solution.py:90
  36.3 1.0 %copy-start.5 = (f32[8,32,1024]{2,1,0:T(8,128)}, f32[8,32,1024]{2,1,0:T(8,128)S(1)}, u32[]{:S(2)}) copy-start(f32[8,32,1024]{2,1,0:T(8,128)S(1)} %get-tuple-element.17) | copy-start | bytes 3145732
  45.1 7.4 %copy-start.4 = (f32[8,32,768]{2,1,0:T(8,128)}, f32[8,32,768]{2,1,0:T(8,128)S(1)}, u32[]{:S(2)}) copy-start(f32[8,32,768]{2,1,0:T(8,128)S(1)} %add_subtract_fusion.1) | copy-start | bytes 2359300
  45.1 6.8 %copy-start.1 = (bf16[768,1024]{1,0:T(8,128)(2,1)S(1)}, bf16[768,1024]{1,0:T(8,128)(2,1)}, u32[]{:S(2)}) copy-start(bf16[768,1024]{1,0:T(8,128)(2,1)} %param.13) | copy-start | bytes 4718596
  46.8 5.7 %copy-start.2 = (f32[8,32,768]{2,1,0:T(8,128)}, f32[8,32,768]{2,1,0:T(8,128)S(1)}, u32[]{:S(2)}) copy-start(f32[8,32,768]{2,1,0:T(8,128)S(1)} %fusion.95) | copy-start | bytes 2359300
  46.8 4.2 %collective-permute-start = (f32[1,32,768]{2,1,0:T(8,128)S(1)}, f32[1,32,768]{2,1,0:T(8,128)S(1)}, u32[]{:S(2)}, u32[]{:S(2)}) collective-permute-start(f32[1,32,768]{2,1,0:T(8,128)S(1)} %slice.46), channel_id=1, source_target_pairs={{0,8},{1,9},{2,10},{3,11},{4,12},{5,13},{6,14},{7,15},{16,24},{17,... | collective-permute-start | bytes 294920 | tf_op jit(solution)/shard_map/ppermute | solution.py:58
  61.4 2.3 %copy-start.3 = (f32[8,32,768]{2,1,0:T(8,128)S(1)}, f32[8,32,768]{2,1,0:T(8,128)}, u32[]{:S(2)}) copy-start(f32[8,32,768]{2,1,0:T(8,128)} %copy-done.2) | copy-start | bytes 2359300
  68.5 7.6 %collective-permute-start.1 = (f32[1,32,768]{2,1,0:T(8,128)S(1)}, f32[1,32,768]{2,1,0:T(8,128)S(1)}, u32[]{:S(2)}, u32[]{:S(2)}) collective-permute-start(f32[1,32,768]{2,1,0:T(8,128)S(1)} %slice.47), channel_id=1, source_target_pairs={{0,8},{1,9},{2,10},{3,11},{4,12},{5,13},{6,14},{7,15},{16,24},{17,... | collective-permute-start | bytes 294920 | tf_op jit(solution)/shard_map/ppermute | solution.py:58
